TPU v7x, 32 devices: a whole 2x2x4 slice. The times are simulated.
32 devices in a mesh: groups: 2 (over y), seq: 8 (over z, x), tp: 2 (over core).
Axes of the slice: x: 2, y: 2, z: 4, core: 2. Of those that a mesh axis runs over, the one named last changes fastest.
Arguments:
- span_queries: bfloat16 [128, 64, 128], P(('groups', 'seq'), 'tp'), parts along dimension 0, may hold values from -180 to 180
- span_keys: bfloat16 [128, 4, 128], P(('groups', 'seq'), 'tp'), parts along dimension 0, may hold values from -9 to 9
- span_values: bfloat16 [128, 4, 128], P(('groups', 'seq'), 'tp'), parts along dimension 0, may hold values from -6.5 to 6.5
- prefix_keys: bfloat16 [1152, 4, 128], P(('groups', 'seq'), 'tp'), parts along dimension 0, may hold values from -9 to 9
- prefix_values: bfloat16 [1152, 4, 128], P(('groups', 'seq'), 'tp'), parts along dimension 0, may hold values from -6.5 to 6.5
- prefix_lengths: int32 [16], P('groups'), parts along dimension 0, may hold values from 1 to 72
- decode_queries: bfloat16 [32, 64, 128], P(('groups', 'seq'), 'tp'), parts along dimension 0, may hold values from -180 to 180
- decode_new_keys: bfloat16 [32, 4, 128], P(('groups', 'seq'), 'tp'), parts along dimension 0, may hold values from -6 to 6
- decode_new_values: bfloat16 [32, 4, 128], P(('groups', 'seq'), 'tp'), parts along dimension 0, may hold values from -6 to 6
- decode_key_cache: bfloat16 [64, 256, 4, 128], P(('groups', 'seq'), None, 'tp'), parts along dimension 0, may hold values from -6 to 6
- decode_value_cache: bfloat16 [64, 256, 4, 128], P(('groups', 'seq'), None, 'tp'), parts along dimension 0, may hold values from -6 to 6
- owner_map: int32 [32, 1], P('groups'), parts along dimension 0, may hold values from 0 to 7; in each aligned block of 16 rows (0 to 15, 16 to 31, ...) at most 4 rows name the same one
- decode_lengths: int32 [32], P('groups'), parts along dimension 0, may hold values from 1 to 256
Outputs:
- prefill_out: bfloat16 [128, 64, 128], P(('groups', 'seq'), 'tp'), parts along dimension 0
- decode_out: bfloat16 [64, 64, 128], P(('groups', 'seq'), 'tp'), parts along dimension 0
There are 2 independent parts, one for each index of `groups`. A program takes and returns all parts, laid end to end along the dimension named above; each array names one. Nothing has to cross between parts.
Inputs may be any that keep to these rules, and one draw needn't show every extreme that they name: `owner_map`: no shard owns more than 4 requests, and some shard owns exactly 4.
All inputs are finite; a program needn't handle non-finite values.
Results may differ from a plain program's by a relative error of at most 0.005.
Values may be sent and summed in bfloat16 or wider, within the bound.
No kernel may reach another device: no remote copies, remote signals or barrier semaphores. Data moves between devices by JAX's collectives and lax.ppermute only.
A program may use at most 64 MiB of HBM per device.

v0:
```python
import jax
import jax.numpy as jnp
from jax import lax
from jax.sharding import PartitionSpec as P

LOWEST = -1e30


def lookup_small(table, wanted):
    columns = jnp.arange(table.shape[0], dtype=jnp.int32)
    return jnp.sum(jnp.where(wanted[:, None] == columns[None, :], table[None, :], 0), axis=1)


def block_split(length):
    blocks = 1
    while length // blocks > 512 or length % blocks != 0:
        blocks += 1
    return blocks


def online_step(carried, queries, key_rows, value_rows, allowed):
    running_max, normalizer, weighted = carried
    scale = queries.shape[-1] ** (-0.5)
    scores = (
        jnp.einsum("tkgd,nkd->tkgn", queries, key_rows, preferred_element_type=jnp.float32) * scale
    )
    visible = allowed[:, None, None, :]
    scores = jnp.where(visible, scores, LOWEST)
    new_max = jnp.maximum(running_max, jnp.max(scores, axis=-1))
    weights = jnp.where(visible, jnp.exp(scores - new_max[..., None]), 0.0)
    factor = jnp.exp(running_max - new_max)
    normalizer = normalizer * factor + jnp.sum(weights, axis=-1)
    weighted = weighted * factor[..., None] + jnp.einsum(
        "tkgn,nkd->tkgd",
        weights.astype(jnp.bfloat16),
        value_rows,
        preferred_element_type=jnp.float32,
    )
    return (new_max, normalizer, weighted)


def guarded_step(carried, queries, key_rows, value_rows, allowed):
    return lax.cond(
        jnp.any(allowed),
        lambda inner: online_step(inner, queries, key_rows, value_rows, allowed),
        lambda inner: inner,
        carried,
    )


def fold_rows(carried, queries, key_rows, value_rows, allowed):
    length = key_rows.shape[0]
    blocks = block_split(length)
    if blocks == 1:
        return guarded_step(carried, queries, key_rows, value_rows, allowed)
    width = length // blocks
    stacked = (
        key_rows.reshape((blocks, width) + key_rows.shape[1:]),
        value_rows.reshape((blocks, width) + value_rows.shape[1:]),
        allowed.reshape(allowed.shape[0], blocks, width).transpose(1, 0, 2),
    )

    def visit(inner_carry, parts):
        return (guarded_step(inner_carry, queries, parts[0], parts[1], parts[2]), None)

    carried, unused = lax.scan(visit, carried, stacked)
    return carried


def on_device(
    span_queries,
    span_keys,
    span_values,
    prefix_keys,
    prefix_values,
    prefix_lengths,
    decode_queries,
    decode_new_keys,
    decode_new_values,
    decode_key_cache,
    decode_value_cache,
    owner_map,
    decode_lengths,
):
    device = lax.axis_index("seq")
    tokens_here, heads_here, head_dim = span_queries.shape
    kv_here = span_keys.shape[1]
    group_size = heads_here // kv_here
    queries = span_queries.reshape(tokens_here, kv_here, group_size, head_dim)
    token_index = device * tokens_here + jnp.arange(tokens_here, dtype=jnp.int32)
    prefix_here = prefix_keys.shape[0]
    initial = (
        jnp.full((tokens_here, kv_here, group_size), LOWEST, jnp.float32),
        jnp.zeros((tokens_here, kv_here, group_size), jnp.float32),
        jnp.zeros((tokens_here, kv_here, group_size, head_dim), jnp.float32),
    )
    stride = prefix_here + tokens_here
    both_keys = jnp.concatenate([prefix_keys, span_keys], axis=0)
    both_values = jnp.concatenate([prefix_values, span_values], axis=0)
    carried = initial
    key_rows = lax.all_gather(both_keys, "seq", axis=0, tiled=True)
    value_rows = lax.all_gather(both_values, "seq", axis=0, tiled=True)
    length = key_rows.shape[0]
    shards = length // stride
    tail = key_rows.shape[1:]
    keys_split = key_rows.reshape((shards, stride) + tail)
    values_split = value_rows.reshape((shards, stride) + tail)
    prefix_k = keys_split[:, :prefix_here].reshape((shards * prefix_here,) + tail)
    prefix_v = values_split[:, :prefix_here].reshape((shards * prefix_here,) + tail)
    span_k = keys_split[:, prefix_here:].reshape((shards * tokens_here,) + tail)
    span_v = values_split[:, prefix_here:].reshape((shards * tokens_here,) + tail)
    prefix_position = jnp.arange(shards * prefix_here, dtype=jnp.int32)
    prefix_ok = prefix_position % prefix_here < lookup_small(
        prefix_lengths, prefix_position // prefix_here
    )
    carried = fold_rows(
        carried,
        queries,
        prefix_k,
        prefix_v,
        jnp.broadcast_to(prefix_ok[None, :], (tokens_here, prefix_k.shape[0])),
    )
    span_position = jnp.arange(shards * tokens_here, dtype=jnp.int32)
    carried = fold_rows(
        carried, queries, span_k, span_v, span_position[None, :] <= token_index[:, None]
    )
    running_max, normalizer, weighted = carried
    prefill_out = (
        (weighted / normalizer[..., None])
        .reshape(tokens_here, heads_here, head_dim)
        .astype(jnp.bfloat16)
    )
    owners = owner_map[:, 0]
    requests = owners.shape[0]
    order = jnp.arange(requests, dtype=jnp.int32)
    earlier = (owners[None, :] == owners[:, None]) & (order[None, :] < order[:, None])
    ranking = jnp.sum(earlier.astype(jnp.int32), axis=1)
    slots_here = decode_key_cache.shape[0]
    slot_ids = jnp.arange(slots_here, dtype=jnp.int32)
    query_rows = lax.all_gather(decode_queries, "seq", axis=0, tiled=True)
    new_keys = lax.all_gather(decode_new_keys, "seq", axis=0, tiled=True)
    new_values = lax.all_gather(decode_new_values, "seq", axis=0, tiled=True)
    chosen = (owners == device)[None, :] & (ranking[None, :] == slot_ids[:, None])
    selector = chosen.astype(jnp.bfloat16)
    picked_queries = jnp.einsum(
        "sn,nhd->shd", selector, query_rows, preferred_element_type=jnp.float32
    )
    picked_keys = jnp.einsum("sn,nkd->skd", selector, new_keys, preferred_element_type=jnp.float32)
    picked_values = jnp.einsum(
        "sn,nkd->skd", selector, new_values, preferred_element_type=jnp.float32
    )
    picked_lengths = jnp.sum(jnp.where(chosen, decode_lengths[None, :], 0), axis=1)
    context = decode_key_cache.shape[1]
    grouped = picked_queries.astype(jnp.bfloat16).reshape(slots_here, kv_here, group_size, head_dim)
    own_keys = picked_keys.astype(jnp.bfloat16)
    own_values = picked_values.astype(jnp.bfloat16)
    scale = head_dim ** (-0.5)
    scores = (
        jnp.einsum("skgd,sckd->skgc", grouped, decode_key_cache, preferred_element_type=jnp.float32)
        * scale
    )
    visible = (jnp.arange(context, dtype=jnp.int32)[None, :] < picked_lengths[:, None])[
        :, None, None, :
    ]
    scores = jnp.where(visible, scores, LOWEST)
    own_score = (
        jnp.einsum("skgd,skd->skg", grouped, own_keys, preferred_element_type=jnp.float32) * scale
    )
    top_score = jnp.maximum(jnp.max(scores, axis=-1), own_score)
    weights = jnp.where(visible, jnp.exp(scores - top_score[..., None]), 0.0)
    own_weight = jnp.exp(own_score - top_score)
    total_weight = jnp.sum(weights, axis=-1) + own_weight
    rounded_own = lax.optimization_barrier(own_weight.astype(jnp.bfloat16)).astype(jnp.float32)
    mixed = jnp.einsum(
        "skgc,sckd->skgd",
        weights.astype(jnp.bfloat16),
        decode_value_cache,
        preferred_element_type=jnp.float32,
    )
    mixed = mixed + rounded_own[..., None] * own_values.astype(jnp.float32)[:, :, None, :]
    count_here = jnp.sum((owners == device).astype(jnp.int32))
    used = (slot_ids < count_here)[:, None, None, None]
    decode_out = (
        jnp.where(used, mixed / total_weight[..., None], 0.0)
        .reshape(slots_here, heads_here, head_dim)
        .astype(jnp.bfloat16)
    )
    return (prefill_out, decode_out)


def solution(mesh):
    return jax.shard_map(
        on_device,
        mesh=mesh,
        in_specs=(
            P(("groups", "seq"), "tp", None),
            P(("groups", "seq"), "tp", None),
            P(("groups", "seq"), "tp", None),
            P(("groups", "seq"), "tp", None),
            P(("groups", "seq"), "tp", None),
            P("groups"),
            P(("groups", "seq"), "tp", None),
            P(("groups", "seq"), "tp", None),
            P(("groups", "seq"), "tp", None),
            P(("groups", "seq"), None, "tp", None),
            P(("groups", "seq"), None, "tp", None),
            P("groups", None),
            P("groups"),
        ),
        out_specs=(P(("groups", "seq"), "tp", None), P(("groups", "seq"), "tp", None)),
        check_vma=False,
    )
```

profile of v0, /device:TPU:0, one launch (start us, length us, event | category | flops | bytes accessed | tf_op | source)
XLA Modules:
  0.0 148.8 jit_solution(11207647977653412298)
XLA Ops:
  0.7 0.7 iota_compare_fusion.3
  2.0 0.7 select_reduce_fusion
  2.9 0.7 copy-done.5
  3.6 32.7 %all_gather.15 = bf16[640,2,128]{2,1,0:T(2,128)(2,1)S(1)} all-gather(bf16[80,2,128]{2,1,0:T(2,128)(2,1)S(1)} %pad_maximum_fusion), channel_id=1, replica_groups=mesh['groups'=2,'seq'=8,'tp'=2] {'seq'}, dimensions={0}, use_global_device_ids=true | all-gather | bytes 368640 | tf_op jit(solution)/shard_map/all_gather | solution.py:101
  36.4 0.8 copy-done.1
  37.2 0.8 copy-done.3
  38.1 30.9 %all_gather.16 = bf16[640,2,128]{2,1,0:T(2,128)(2,1)S(1)} all-gather(bf16[80,2,128]{2,1,0:T(2,128)(2,1)S(1)} %pad_maximum_fusion.1), channel_id=1, replica_groups=mesh['groups'=2,'seq'=8,'tp'=2] {'seq'}, dimensions={0}, use_global_device_ids=true | all-gather | bytes 368640 | tf_op jit(solution)/shard_map/all_gather | solution.py:102
  69.1 4.4 %while.14 = (s32[]{:T(128)}, f32[8,2,16]{2,0,1:T(8,128)S(1)}, f32[8,2,16]{2,0,1:T(8,128)S(1)}, f32[8,2,16,128]{3,2,0,1:T(8,128)S(1)}, pred[2,8,288]{2,1,0:T(8,12...) while((s32[]{:T(128)}, f32[8,2,16]{2,0,1:T(8,128)S(1)}, ...), condition=%wide.region_8.9_spmd, body=%wide.region_2.8_spmd.sunk | while | flops 38480640 | bytes 1649647 | solution.py:66
  69.2 0.7 fusion.72
  70.5 0.9 conditional.4
  70.5 0.3 fusion.67
  70.8 0.2 fusion.4
  71.1 0.3 fusion.2
  71.4 0.7 fusion.72
  72.7 0.9 conditional.4
  72.7 0.3 fusion.67
  73.3 0.3 fusion.2
  73.6 0.7 conditional.2
  73.6 0.3 fusion.68
  74.1 0.2 fusion.16
  74.5 0.6 copy.71
  75.2 30.5 %all_gather.17 = bf16[16,32,128]{2,1,0:T(8,128)(2,1)S(1)} all-gather(bf16[2,32,128]{2,1,0:T(8,128)(2,1)S(1)} %copy-done.4), channel_id=1, replica_groups=mesh['groups'=2,'seq'=8,'tp'=2] {'seq'}, dimensions={0}, use_global_device_ids=true | all-gather | bytes 147456 | tf_op jit(solution)/shard_map/all_gather | solution.py:140
  105.7 0.7 copy-done.10
  106.5 0.6 convert_reduce_fusion.1
  107.2 0.7 copy-done.9
  108.2 0.3 fusion.69
  108.5 0.7 copy-done.7
  109.2 20.5 %all_gather.18 = bf16[16,2,128]{2,1,0:T(2,128)(2,1)S(1)} all-gather(bf16[2,2,128]{2,1,0:T(2,128)(2,1)S(1)} %copy-done.7), channel_id=1, replica_groups=mesh['groups'=2,'seq'=8,'tp'=2] {'seq'}, dimensions={0}, use_global_device_ids=true | all-gather | bytes 9216 | tf_op jit(solution)/shard_map/all_gather | solution.py:141
  130.2 0.7 copy-done.8
  130.8 16.3 %all_gather.19 = bf16[16,2,128]{2,1,0:T(2,128)(2,1)S(1)} all-gather(bf16[2,2,128]{2,1,0:T(2,128)(2,1)S(1)} %copy-done.8), channel_id=1, replica_groups=mesh['groups'=2,'seq'=8,'tp'=2] {'seq'}, dimensions={0}, use_global_device_ids=true | all-gather | bytes 9216 | tf_op jit(solution)/shard_map/all_gather | solution.py:142
  147.2 0.6 iota_compare_fusion.5
  147.9 0.9 fusion.34
  (57 shorter events, 2.2 us)
Async XLA Ops:
  0.6 107.6 %copy-start = (bf16[4,256,2,128]{3,2,1,0:T(2,128)(2,1)S(1)}, bf16[4,256,2,128]{3,2,1,0:T(2,128)(2,1)}, u32[]{:S(2)}) copy-start(bf16[4,256,2,128]{3,2,1,0:T(2,128)(2,1)} %param.28) | copy-start | bytes 1572868
  0.6 2.3 %copy-start.2 = (bf16[72,2,128]{2,1,0:T(2,128)(2,1)S(1)}, bf16[72,2,128]{2,1,0:T(2,128)(2,1)}, u32[]{:S(2)}) copy-start(bf16[72,2,128]{2,1,0:T(2,128)(2,1)} %param.22) | copy-start | bytes 110596
  2.9 0.7 copy-start.5
  36.4 0.8 copy-start.1
  37.2 0.8 copy-start.3
  37.2 0.8 copy-start.6
  74.5 0.7 copy-start.4
  105.7 0.7 copy-start.10
  107.2 0.7 copy-start.9
  108.1 39.8 %copy-start.11 = (bf16[4,256,2,128]{3,2,1,0:T(2,128)(2,1)S(1)}, bf16[4,256,2,128]{3,2,1,0:T(2,128)(2,1)}, u32[]{:S(2)}) copy-start(bf16[4,256,2,128]{3,2,1,0:T(2,128)(2,1)} %param.29) | copy-start | bytes 1572868
  108.5 0.7 copy-start.7
  130.1 0.7 copy-start.8
where the time goes:
time: 149 us
  blocking collectives  131 us (88%)
  local copies, waits for them, and re-layouts  5.93 us (4%)
  other arithmetic  5.57 us (4%)
  matrix products  3.39 us (2%)
  between operations  1.53 us (1%)
  loops' own time  1.5 us (1%)
    all_gather x1, blocking collectives, on_device(): key_rows = lax.all_gather(both_keys, 'seq', axis=0, tiled=True)  32.7 us
    all_gather x1, blocking collectives, on_device(): value_rows = lax.all_gather(both_values, 'seq', axis=0, tiled=True)  30.9 us
    all_gather x1, blocking collectives, on_device(): query_rows = lax.all_gather(decode_queries, 'seq', axis=0, tiled=True)  30.5 us
    all_gather x1, blocking collectives, on_device(): new_keys = lax.all_gather(decode_new_keys, 'seq', axis=0, tiled=True)  20.5 us
    all_gather x1, blocking collectives, on_device(): new_values = lax.all_gather(decode_new_values, 'seq', axis=0, tiled=True)  16.3 us
    unnamed x24, local copies, waits for them, and re-layouts  4.99 us

commit v1 on v0

--- a/solution.py
+++ b/solution.py
@@ -137,8 +137,13 @@
     ranking = jnp.sum(earlier.astype(jnp.int32), axis=1)
     slots_here = decode_key_cache.shape[0]
     slot_ids = jnp.arange(slots_here, dtype=jnp.int32)
-    query_rows = lax.all_gather(decode_queries, "seq", axis=0, tiled=True)
-    new_keys = lax.all_gather(decode_new_keys, "seq", axis=0, tiled=True)
+    query_rows, new_keys = jnp.split(
+        lax.all_gather(
+            jnp.concatenate([decode_queries, decode_new_keys], axis=1), "seq", axis=0, tiled=True
+        ),
+        [decode_queries.shape[1]],
+        axis=1,
+    )
     new_values = lax.all_gather(decode_new_values, "seq", axis=0, tiled=True)
     chosen = (owners == device)[None, :] & (ranking[None, :] == slot_ids[:, None])
     selector = chosen.astype(jnp.bfloat16)

time: 149 us -> 133 us (0.89)
  blocking collectives: 131 us -> 115 us
    all_gather x2 -> x1, blocking collectives: 51 us -> 30.6 us  [on_device(): lax.all_gather(jnp.concatenate([decode_queries, decode_new_keys], axis=1)...]
    all_gather x1, blocking collectives: 16.3 us -> 20.8 us  [on_device(): new_values = lax.all_gather(decode_new_values, 'seq', axis=0, tiled=True)]
where the time goes in v1:
time: 133 us
  blocking collectives  115 us (86%)
  local copies, waits for them, and re-layouts  5.86 us (4%)
  other arithmetic  5.58 us (4%)
  matrix products  3.39 us (3%)
  between operations  1.55 us (1%)
  loops' own time  1.5 us (1%)
    all_gather x1, blocking collectives, on_device(): key_rows = lax.all_gather(both_keys, 'seq', axis=0, tiled=True)  32.7 us
    all_gather x1, blocking collectives, on_device(): value_rows = lax.all_gather(both_values, 'seq', axis=0, tiled=True)  30.9 us
    all_gather x1, blocking collectives, on_device(): lax.all_gather(jnp.concatenate([decode_queries, decode_new_keys], axis=1)...  30.6 us
    all_gather x1, blocking collectives, on_device(): new_values = lax.all_gather(decode_new_values, 'seq', axis=0, tiled=True)  20.8 us
    unnamed x24, local copies, waits for them, and re-layouts  4.91 us

profile of v1, /device:TPU:0, one launch (start us, length us, event | category | flops | bytes accessed | tf_op | source)
XLA Modules:
  0.0 132.7 jit_solution(17880415615157189352)
XLA Ops:
  0.7 0.7 iota_compare_fusion.3
  2.0 0.7 select_reduce_fusion
  2.9 0.7 copy-done.5
  3.6 32.7 %all_gather.12 = bf16[640,2,128]{2,1,0:T(2,128)(2,1)S(1)} all-gather(bf16[80,2,128]{2,1,0:T(2,128)(2,1)S(1)} %pad_maximum_fusion), channel_id=1, replica_groups=mesh['groups'=2,'seq'=8,'tp'=2] {'seq'}, dimensions={0}, use_global_device_ids=true | all-gather | bytes 368640 | tf_op jit(solution)/shard_map/all_gather | solution.py:101
  36.4 0.8 copy-done.1
  37.2 0.8 copy-done.3
  38.1 30.9 %all_gather.13 = bf16[640,2,128]{2,1,0:T(2,128)(2,1)S(1)} all-gather(bf16[80,2,128]{2,1,0:T(2,128)(2,1)S(1)} %pad_maximum_fusion.1), channel_id=1, replica_groups=mesh['groups'=2,'seq'=8,'tp'=2] {'seq'}, dimensions={0}, use_global_device_ids=true | all-gather | bytes 368640 | tf_op jit(solution)/shard_map/all_gather | solution.py:102
  69.1 4.4 %while.14 = (s32[]{:T(128)}, f32[8,2,16]{2,0,1:T(8,128)S(1)}, f32[8,2,16]{2,0,1:T(8,128)S(1)}, f32[8,2,16,128]{3,2,0,1:T(8,128)S(1)}, pred[2,8,288]{2,1,0:T(8,12...) while((s32[]{:T(128)}, f32[8,2,16]{2,0,1:T(8,128)S(1)}, ...), condition=%wide.region_8.9_spmd, body=%wide.region_2.8_spmd.sunk | while | flops 38480640 | bytes 1649647 | solution.py:66
  69.1 0.7 fusion.72
  70.4 0.9 conditional.4
  70.4 0.3 fusion.67
  70.7 0.2 fusion.4
  71.0 0.3 fusion.2
  71.3 0.7 fusion.72
  72.6 0.9 conditional.4
  72.6 0.3 fusion.67
  72.9 0.2 fusion.4
  73.2 0.3 fusion.2
  73.5 0.7 conditional.2
  73.5 0.3 fusion.68
  74.0 0.2 fusion.16
  74.4 0.6 copy.73
  75.1 0.6 copy-done.7
  75.7 30.6 %all_gather.14 = bf16[16,34,128]{2,1,0:T(8,128)(2,1)S(1)} all-gather(bf16[2,34,128]{2,1,0:T(8,128)(2,1)S(1)} %pad_maximum_fusion.2), channel_id=1, replica_groups=mesh['groups'=2,'seq'=8,'tp'=2] {'seq'}, dimensions={0}, use_global_device_ids=true | all-gather | bytes 156672 | tf_op jit(solution)/shard_map/all_gather | solution.py:141
  106.3 0.6 copy-done.10
  107.1 0.6 convert_reduce_fusion.1
  107.8 0.7 copy-done.9
  108.8 0.3 fusion.69
  109.6 0.7 copy-done.8
  110.3 20.8 %all_gather.15 = bf16[16,2,128]{2,1,0:T(2,128)(2,1)S(1)} all-gather(bf16[2,2,128]{2,1,0:T(2,128)(2,1)S(1)} %copy-done.8), channel_id=1, replica_groups=mesh['groups'=2,'seq'=8,'tp'=2] {'seq'}, dimensions={0}, use_global_device_ids=true | all-gather | bytes 9216 | tf_op jit(solution)/shard_map/all_gather | solution.py:147
  131.2 0.6 iota_compare_fusion.5
  131.9 0.9 fusion.34
  (59 shorter events, 2.1 us)
Async XLA Ops:
  0.6 108.2 %copy-start = (bf16[4,256,2,128]{3,2,1,0:T(2,128)(2,1)S(1)}, bf16[4,256,2,128]{3,2,1,0:T(2,128)(2,1)}, u32[]{:S(2)}) copy-start(bf16[4,256,2,128]{3,2,1,0:T(2,128)(2,1)} %param.28) | copy-start | bytes 1572868
  0.6 2.3 %copy-start.2 = (bf16[72,2,128]{2,1,0:T(2,128)(2,1)S(1)}, bf16[72,2,128]{2,1,0:T(2,128)(2,1)}, u32[]{:S(2)}) copy-start(bf16[72,2,128]{2,1,0:T(2,128)(2,1)} %param.22) | copy-start | bytes 110596
  2.9 0.7 copy-start.5
  36.4 0.8 copy-start.1
  37.2 0.8 copy-start.3
  37.2 0.8 copy-start.6
  74.4 0.7 copy-start.4
  75.0 0.7 copy-start.7
  106.3 0.7 copy-start.10
  107.8 0.7 copy-start.9
  108.7 23.2 %copy-start.11 = (bf16[4,256,2,128]{3,2,1,0:T(2,128)(2,1)S(1)}, bf16[4,256,2,128]{3,2,1,0:T(2,128)(2,1)}, u32[]{:S(2)}) copy-start(bf16[4,256,2,128]{3,2,1,0:T(2,128)(2,1)} %param.29) | copy-start | bytes 1572868
  109.6 0.7 copy-start.8
